TPU v7x, 32 devices: a whole 2x2x4 slice. The times are simulated.
32 devices in a mesh: section: 4 (over y, core), expert: 2 (over x), tensor: 4 (over z).
Axes of the slice: x: 2, y: 2, z: 4, core: 2. Of those that a mesh axis runs over, the one named last changes fastest.
Arguments:
- branch_weights: bfloat16 [2, 8192, 8192], P('expert', ('section', 'tensor')), may hold values from -0.125 to 0.125
- branch_gains: float32 [2, 8192], P('expert', ('section', 'tensor')), may hold values from 0.1 to 1.9
- column_order: int32 [2, 8192], P('expert'), may hold values from 0 to 8191, each once within a row
- layer_order: int32 [4], replicated, may hold values from 0 to 3, each once
- probe_seeds: int32 [1024], replicated, may hold values from 1 to 32767
Outputs:
- expert_weights: bfloat16 [2, 8192, 8192], P('expert', None, ('section', 'tensor'))
- checksum: float32 [2, 1024, 8192], P('expert', None, ('section', 'tensor'))
- fingerprint: float32 [2, 1024], P('expert')
- shared_gain: float32 [8192], replicated
Inputs may be any that keep to these rules, and one draw needn't show every extreme that they name: Each row of column_order names every hidden unit once. layer_order names every layer once.
All inputs are finite; a program needn't handle non-finite values.
Results may differ from a plain program's by a relative error of at most 0.0034.
Values may be sent and summed in bfloat16 or wider, within the bound.
A program may use at most 64 MiB of HBM per device.

v0:
```python
import jax
import jax.numpy as jnp
from jax import lax
from jax.sharding import PartitionSpec as P

D = 2048
FF = 8192


def probe_at(probe_seeds, row_ids):
    hashed = probe_seeds[:, None] * (row_ids[None, :] + 1) % 65521
    return (hashed % 511 - 255).astype(jnp.float32) / 256.0


def sketch(natural, probe_seeds):
    segment_rows = D // 2
    running = jnp.zeros((probe_seeds.shape[0], natural.shape[1]), jnp.float32)
    for portion in range(natural.shape[0] // segment_rows):
        row_ids = portion * segment_rows + lax.iota(jnp.int32, segment_rows)
        probes = probe_at(probe_seeds, row_ids).astype(jnp.bfloat16)
        running = running + jnp.dot(
            probes,
            natural[portion * segment_rows : (portion + 1) * segment_rows],
            preferred_element_type=jnp.float32,
        )
    return running


def local(branch_weights, branch_gains, column_order, layer_order, probe_seeds):
    weights = branch_weights[0]
    rows_dev = weights.shape[0]
    n_section = lax.axis_size("section")
    n_tensor = lax.axis_size("tensor")
    groups = n_section * n_tensor
    cols_dev = weights.shape[1] // groups
    layers = layer_order.shape[0]
    own_gains = branch_gains[0]
    mean_gains = lax.psum(own_gains, "expert") / lax.axis_size("expert")
    scaling = own_gains / mean_gains
    permuted = jnp.take(weights, column_order[0], axis=1)
    folded = (permuted.astype(jnp.float32) * scaling[:, None]).astype(jnp.bfloat16)
    per_layer = D // rows_dev
    slot_ids = lax.iota(jnp.int32, layers)
    inverse = jnp.sum(
        jnp.where(layer_order[None, :] == slot_ids[:, None], slot_ids[None, :], 0), axis=1
    )
    block_ids = lax.iota(jnp.int32, groups)
    layer_ids = block_ids // per_layer
    source_pos = (
        jnp.sum(jnp.where(layer_ids[:, None] == slot_ids[None, :], inverse[None, :], 0), axis=1)
        * per_layer
        + block_ids % per_layer
    )
    all_gains = lax.all_gather(mean_gains, ("section", "tensor"), axis=0, tiled=True)
    shared_gain = all_gains.reshape(groups, rows_dev)[source_pos].reshape(groups * rows_dev)
    device = lax.axis_index(("section", "tensor"))
    seven = jnp.full((1,), 7919, jnp.int32)
    arrived = lax.all_to_all(
        folded.reshape(rows_dev, groups, cols_dev),
        ("section", "tensor"),
        split_axis=1,
        concat_axis=0,
        tiled=True,
    )
    width_cols = arrived.shape[2]
    ordered = arrived.reshape(groups, rows_dev, width_cols)[source_pos].reshape(
        groups * rows_dev, width_cols
    )
    sketches = sketch(ordered, probe_seeds)
    column_probe = probe_at(seven, device * cols_dev + lax.iota(jnp.int32, cols_dev))[0]
    partial_print = jnp.dot(sketches, column_probe, precision=lax.Precision.HIGHEST)
    fingerprint = lax.psum(partial_print, ("section", "tensor")) * FF ** (-0.5)
    return (ordered[None], sketches[None], fingerprint[None], shared_gain)


def solution(mesh):
    return jax.shard_map(
        local,
        mesh=mesh,
        in_specs=(
            P("expert", ("section", "tensor"), None),
            P("expert", ("section", "tensor")),
            P("expert", None),
            P(),
            P(),
        ),
        out_specs=(
            P("expert", None, ("section", "tensor")),
            P("expert", None, ("section", "tensor")),
            P("expert", None),
            P(),
        ),
        check_vma=False,
    )
```

profile of v0, /device:TPU:0, one launch (start us, length us, event | category | flops | bytes accessed | tf_op | source)
XLA Modules:
  0.0 383.8 jit_solution(6322284176018858667)
XLA Ops:
  0.6 6.0 %psum.14 = f32[512]{0:T(512)S(1)} all-reduce(f32[512]{0:T(512)} %bitcast.67), channel_id=1, replica_groups=mesh['section'=4,'expert'=2,'tensor'=4] {'expert'}, use_global_device_ids=true, to_apply=%region_0.0 | all-reduce | flops 512 | bytes 4096 | tf_op jit(solution)/shard_map/psum | solution.py:38
  6.6 0.7 broadcast_multiply_fusion.1
  7.3 11.9 %copy.16 = bf16[1,512,8192]{1,2,0:T(8,128)(2,1)} copy(bf16[1,512,8192]{2,1,0:T(8,128)(2,1)} %param.5) | data formatting | bytes 16777216 | tf_op args[0]
  19.3 0.0 copy-done.1
  19.3 38.2 %gather_fusion = bf16[8192,512]{1,0:T(8,128)(2,1)} fusion(bf16[512,8192]{0,1:T(8,128)(2,1)} %bitcast.48, s32[8192]{0:T(1024)S(1)} %broadcast_clamp_fusion), kind=kCustom, calls=%fused_computation | custom fusion | bytes 16809984 | tf_op jit(solution)/shard_map/jit(_take)/gather | solution.py:40
  57.6 12.3 %copy.17 = bf16[512,16,512]{2,0,1:T(8,128)(2,1)} copy(bf16[512,16,512]{0,2,1:T(8,128)(2,1)} %bitcast.49) | data formatting | bytes 16777216 | tf_op jit(solution)/shard_map/jit(_take)/gather | solution.py:40
  69.8 0.5 broadcast.368
  70.3 0.7 reduce.3
  71.1 9.0 %multiply_convert_fusion = bf16[512,16,512]{2,0,1:T(8,128)(2,1)} fusion(f32[512]{0:T(512)S(1)} %get-tuple-element.13, bf16[512,16,512]{2,0,1:T(8,128)(2,1)} %copy.17, pred[16,512]{1,0:T(8,128)(4,1)S(1)} %compare_and_fusion), kind=kLoop, calls=%fused_computation.3 | loop fusion | flops 16777216 | bytes 16787456 | tf_op jit(solution)/shard_map/convert_element_type | solution.py:41
  80.1 6.7 %all-to-all-start = ((bf16[512,16,512]{2,0,1:T(8,128)(2,1)}), bf16[512,16,512]{2,0,1:T(8,128)(2,1)}, u32[]{:S(2)}, u32[]{:S(2)}) async-start(bf16[512,16,512]{2,0,1:T(8,128)(2,1)} %multiply_convert_fusion), calls=%async_computation | async-start | bytes 16777216 | tf_op jit(solution)/shard_map/all_to_all | solution.py:58
  86.7 207.0 %all-gather = f32[16,1,512]{2,1,0:T(1,128)S(1)} all-gather(f32[1,1,512]{2,1,0:T(1,128)S(1)} %bitcast.66), channel_id=1, replica_groups=mesh['section'=4,'expert'=2,'tensor'=4] {'section','tensor'}, dimensions={0}, use_global_device_ids=true | all-gather | bytes 34816 | tf_op jit(solution)/shard_map/all_gather | solution.py:54
  293.7 0.0 copy-done.3
  293.7 0.1 select_reduce_fusion.1
  293.9 0.1 select_reduce_fusion
  294.0 0.6 gather_fusion.2
  294.5 0.6 copy.19
  295.3 0.0 all-to-all-done
  295.3 8.3 %gather_fusion.1 = bf16[16,512,512]{2,1,0:T(8,128)(2,1)} fusion(bf16[16,512,512]{2,1,0:T(8,128)(2,1)} %bitcast.8, s32[1024]{0:T(1024)S(1)} %pad_clamp_fusion), kind=kCustom, calls=%fused_computation.1 | custom fusion | bytes 16777280 | tf_op jit(solution)/shard_map/gather | solution.py:66
  303.6 4.1 %fusion.212 = (bf16[2,512,512]{2,1,0:T(8,128)(2,1)S(1)}, bf16[2,512,512]{2,1,0:T(8,128)(2,1)S(1)}, bf16[2,512,512]{2,1,0:T(8,128)(2,1)S(1)}, bf16[2,512,512]{2,1...) fusion(bf16[16,512,512]{2,1,0:T(8,128)(2,1)} %gather_fusion.1), kind=kLoop, calls=%fused_computation.260 | loop fusion | bytes 16777216 | tf_op jit(solution)/shard_map/slice | solution.py:23
  307.7 5.3 %fusion.100 = f32[1024,512]{1,0:T(8,128)S(1)} fusion(bf16[1024,512]{1,0:T(8,128)(2,1)S(1)} %bitcast.60, s32[1024]{0:T(1024)S(1)} %iota_add_fusion.6, s32[1024]{0:T(1024)S(1)} %copy-done.2), kind=kOutput, calls=%fused_computation.122 | convolution fusion | flops 1091567616 | bytes 3153920 | tf_op jit(solution)/shard_map/dot_general | solution.py:21
  313.0 5.3 %fusion.88 = f32[1024,512]{1,0:T(8,128)S(1)} fusion(bf16[1024,512]{1,0:T(8,128)(2,1)S(1)} %bitcast.59, s32[1024]{0:T(1024)S(1)} %iota_add_fusion, s32[1024]{0:T(1024)S(1)} %copy-done.2), kind=kOutput, calls=%fused_computation.116 | convolution fusion | flops 1091567616 | bytes 3153920 | tf_op jit(solution)/shard_map/dot_general | solution.py:21
  318.3 5.5 %fusion.90 = f32[1024,512]{1,0:T(8,128)S(1)} fusion(bf16[1024,512]{1,0:T(8,128)(2,1)S(1)} %bitcast.58, s32[1024]{0:T(1024)S(1)} %iota_add_fusion.1, s32[1024]{0:T(1024)S(1)} %copy-done.2), kind=kOutput, calls=%fused_computation.117 | convolution fusion | flops 1091567616 | bytes 3153920 | tf_op jit(solution)/shard_map/dot_general | solution.py:21
  323.7 5.3 %fusion.92 = f32[1024,512]{1,0:T(8,128)S(1)} fusion(bf16[1024,512]{1,0:T(8,128)(2,1)S(1)} %bitcast.57, s32[1024]{0:T(1024)S(1)} %iota_add_fusion.2, s32[1024]{0:T(1024)S(1)} %copy-done.2), kind=kOutput, calls=%fused_computation.118 | convolution fusion | flops 1091567616 | bytes 3153920 | tf_op jit(solution)/shard_map/dot_general | solution.py:21
  329.0 5.7 %fusion.94 = f32[1024,512]{1,0:T(8,128)S(1)} fusion(bf16[1024,512]{1,0:T(8,128)(2,1)S(1)} %bitcast.56, s32[1024]{0:T(1024)S(1)} %iota_add_fusion.3, s32[1024]{0:T(1024)S(1)} %copy-done.2), kind=kOutput, calls=%fused_computation.119 | convolution fusion | flops 1091567616 | bytes 3153920 | tf_op jit(solution)/shard_map/dot_general | solution.py:21
  334.7 5.3 %fusion.96 = f32[1024,512]{1,0:T(8,128)S(1)} fusion(bf16[1024,512]{1,0:T(8,128)(2,1)S(1)} %bitcast.55, s32[1024]{0:T(1024)S(1)} %iota_add_fusion.4, s32[1024]{0:T(1024)S(1)} %copy-done.2), kind=kOutput, calls=%fused_computation.120 | convolution fusion | flops 1091567616 | bytes 3153920 | tf_op jit(solution)/shard_map/dot_general | solution.py:21
  340.0 5.5 %fusion.98 = f32[1024,512]{1,0:T(8,128)S(1)} fusion(bf16[1024,512]{1,0:T(8,128)(2,1)S(1)} %bitcast.54, s32[1024]{0:T(1024)S(1)} %iota_add_fusion.5, s32[1024]{0:T(1024)S(1)} %copy-done.2), kind=kOutput, calls=%fused_computation.121 | convolution fusion | flops 1091567616 | bytes 3153920 | tf_op jit(solution)/shard_map/dot_general | solution.py:21
  345.5 6.0 %add_add_fusion = f32[1024,512]{1,0:T(8,128)S(1)} fusion(f32[1024,512]{1,0:T(8,128)S(1)} %fusion.88, f32[1024,512]{1,0:T(8,128)S(1)} %fusion.90, f32[1024,512]{1,0:T(8,128)S(1)} %fusion.92, f32[1024,512]{1,0:T(8,128)S(1)} %fusion.94, f32[1024,512]{1,0:T(8,128)S(1)} %fusion.96, f32[1024,512]{1,0:T(8,128)S(1)} %fusion.98, f32[1024,512]{1,0:T(8,128)S(1)} %fusion.100, ...), kind=kOutput, calls=%fused_computation.125 | convolution fusion | flops 1095237632 | bytes 17833984 | tf_op jit(solution)/shard_map/dot_general | solution.py:21
  351.5 0.0 copy-start
  351.5 1.9 fusion.213
  353.4 29.7 %psum.15 = f32[1024]{0:T(1024)S(1)} all-reduce(f32[1024]{0:T(1024)S(1)} %bitcast.64), channel_id=1, replica_groups=mesh['section'=4,'expert'=2,'tensor'=4] {'section','tensor'}, use_global_device_ids=true, to_apply=%region_3.4 | all-reduce | flops 1024 | bytes 8192 | tf_op jit(solution)/shard_map/psum | solution.py:72
  383.1 0.6 broadcast_multiply_fusion
  383.7 0.0 copy-done
  (21 shorter events, 0.2 us)
Async XLA Ops:
  7.3 11.9 %copy-start.1 = (s32[1,8192]{1,0:T(1,128)S(1)}, s32[1,8192]{1,0:T(1,128)}, u32[]{:S(2)}) copy-start(s32[1,8192]{1,0:T(1,128)} %param.7) | copy-start | bytes 98308
  80.1 213.7 %copy-start.3 = (s32[4]{0:T(128)S(1)}, s32[4]{0:T(128)}, u32[]{:S(2)}) copy-start(s32[4]{0:T(128)} %param.8) | copy-start | bytes 52
  80.1 215.2 %all-to-all-start = ((bf16[512,16,512]{2,0,1:T(8,128)(2,1)}), bf16[512,16,512]{2,0,1:T(8,128)(2,1)}, u32[]{:S(2)}, u32[]{:S(2)}) async-start(bf16[512,16,512]{2,0,1:T(8,128)(2,1)} %multiply_convert_fusion), calls=%async_computation | async-start | bytes 16777216 | tf_op jit(solution)/shard_map/all_to_all | solution.py:58
  303.6 4.1 %copy-start.2 = (s32[1024]{0:T(1024)S(1)}, s32[1024]{0:T(1024)}, u32[]{:S(2)}) copy-start(s32[1024]{0:T(1024)} %param.9) | copy-start | bytes 12292
  351.5 32.2 %copy-start = (f32[1024,512]{1,0:T(8,128)}, f32[1024,512]{1,0:T(8,128)S(1)}, u32[]{:S(2)}) copy-start(f32[1024,512]{1,0:T(8,128)S(1)} %add_add_fusion) | copy-start | bytes 6291460
where the time goes:
time: 390 us; the launch traced here: 384 us
  blocking collectives  243 us (62%)
  local copies, waits for them, and re-layouts  76.6 us (20%)
  matrix products  45.7 us (12%)
  other arithmetic  11.3 us (3%)
  starting transfers between devices  6.66 us (2%)
    all_gather x1, blocking collectives, local(): lax.all_gather(mean_gains, ('section', 'tensor'), axis=0, tiled=True)  207 us
    gather x2, local copies, waits for them, and re-layouts, local(): permuted = jnp.take(weights, column_order[0], axis=1)  50.5 us
    dot_general x8, matrix products, sketch(): jnp.dot(probes, natural[portion * segment_rows:(portion + 1) * segment_ro...  43.8 us
    psum x1, blocking collectives, local(): fingerprint = lax.psum(partial_print, ('section', 'tensor')) * FF ** (-0.5)  29.7 us
    unnamed x12, local copies, waits for them, and re-layouts  13.1 us
    convert_element_type x1, other arithmetic, local(): (permuted.astype(jnp.float32) * scaling[:, None]).astype(jnp.bfloat16)  8.97 us
    gather x1, local copies, waits for them, and re-layouts, local(): arrived.reshape(groups, rows_dev, width_cols)[source_pos]  8.32 us
  transfers between devices with their start and end apart: 1, of which 0 were waited for; matrix products, arithmetic and copies ran while one was open for 0% of the time, Pallas kernels for 0%

commit v1 on v0

--- a/solution.py
+++ b/solution.py
@@ -51,7 +51,8 @@
         * per_layer
         + block_ids % per_layer
     )
-    all_gains = lax.all_gather(mean_gains, ("section", "tensor"), axis=0, tiled=True)
+    repeated = jnp.stack([mean_gains] * lax.axis_size(("section", "tensor")))
+    all_gains = jnp.concatenate(lax.all_to_all(repeated, ("section", "tensor"), 0, 0), axis=0)
     shared_gain = all_gains.reshape(groups, rows_dev)[source_pos].reshape(groups * rows_dev)
     device = lax.axis_index(("section", "tensor"))
     seven = jnp.full((1,), 7919, jnp.int32)

time: 390 us -> 374 us (0.959)
  blocking collectives: 243 us -> 37.4 us
  waiting for transfers between devices: 0.01 us -> 183 us
  starting transfers between devices: 6.66 us -> 12.7 us
    all_gather x1 -> x0, blocking collectives: 207 us -> none  [local(): lax.all_gather(mean_gains, ('section', 'tensor'), axis=0, tiled=True)]
    all_to_all x1, waiting for transfers between devices: 0.01 us -> 183 us  [local(): lax.all_to_all(folded.reshape(rows_dev, groups, cols_dev), ('section', 't...]
    all_to_all x0 -> x1, starting transfers between devices: none -> 6.48 us  [local(): lax.all_to_all(repeated, ('section', 'tensor'), 0, 0)]
  transfers between devices with their start and end apart: 1 -> 2, of which waited for: 0 -> 1; matrix products, arithmetic and copies ran while one was open for 0% -> 20% of each run, Pallas kernels for 0% -> 0%
where the time goes in v1:
time: 374 us; the launch traced here: 368 us
  waiting for transfers between devices  183 us (49%)
  local copies, waits for them, and re-layouts  77.2 us (21%)
  matrix products  45.7 us (12%)
  blocking collectives  37.4 us (10%)
  starting transfers between devices  12.7 us (3%)
  other arithmetic  11.3 us (3%)
    all_to_all x1, waiting for transfers between devices, local(): lax.all_to_all(folded.reshape(rows_dev, groups, cols_dev), ('section', 't...  183 us
    gather x2, local copies, waits for them, and re-layouts, local(): permuted = jnp.take(weights, column_order[0], axis=1)  50.5 us
    dot_general x8, matrix products, sketch(): jnp.dot(probes, natural[portion * segment_rows:(portion + 1) * segment_ro...  43.8 us
    psum x1, blocking collectives, local(): fingerprint = lax.psum(partial_print, ('section', 'tensor')) * FF ** (-0.5)  31.4 us
    unnamed x12, local copies, waits for them, and re-layouts  13.1 us
    convert_element_type x1, other arithmetic, local(): (permuted.astype(jnp.float32) * scaling[:, None]).astype(jnp.bfloat16)  8.97 us
    gather x1, local copies, waits for them, and re-layouts, local(): arrived.reshape(groups, rows_dev, width_cols)[source_pos]  8.32 us
  transfers between devices with their start and end apart: 2, of which 1 were waited for; matrix products, arithmetic and copies ran while one was open for 20% of the time, Pallas kernels for 0%

profile of v1, /device:TPU:0, one launch (start us, length us, event | category | flops | bytes accessed | tf_op | source)
XLA Modules:
  0.0 367.8 jit_solution(7823173047653040114)
XLA Ops:
  0.6 6.0 %psum.14 = f32[512]{0:T(512)S(1)} all-reduce(f32[512]{0:T(512)} %bitcast.65), channel_id=1, replica_groups=mesh['section'=4,'expert'=2,'tensor'=4] {'expert'}, use_global_device_ids=true, to_apply=%region_0.0 | all-reduce | flops 512 | bytes 4096 | tf_op jit(solution)/shard_map/psum | solution.py:38
  6.6 0.7 broadcast_multiply_fusion.1
  7.3 0.6 stack.2
  8.0 6.5 %all-to-all-start.1 = ((f32[16,1,512]{2,1,0:T(1,128)}), f32[16,1,512]{2,1,0:T(1,128)S(1)}, u32[]{:S(2)}, u32[]{:S(2)}) async-start(f32[16,1,512]{2,1,0:T(1,128)} %stack.2), calls=%async_computation.1 | async-start | bytes 65536 | tf_op jit(solution)/shard_map/all_to_all | solution.py:55
  14.4 0.0 copy-start.1
  14.5 11.9 %copy.16 = bf16[1,512,8192]{1,2,0:T(8,128)(2,1)} copy(bf16[1,512,8192]{2,1,0:T(8,128)(2,1)} %param.5) | data formatting | bytes 16777216 | tf_op args[0]
  26.4 38.2 %gather_fusion = bf16[8192,512]{1,0:T(8,128)(2,1)} fusion(bf16[512,8192]{0,1:T(8,128)(2,1)} %bitcast.47, s32[8192]{0:T(1024)S(1)} %broadcast_clamp_fusion), kind=kCustom, calls=%fused_computation | custom fusion | bytes 16809984 | tf_op jit(solution)/shard_map/jit(_take)/gather | solution.py:40
  64.7 12.3 %copy.17 = bf16[512,16,512]{2,0,1:T(8,128)(2,1)} copy(bf16[512,16,512]{0,2,1:T(8,128)(2,1)} %bitcast.48) | data formatting | bytes 16777216 | tf_op jit(solution)/shard_map/jit(_take)/gather | solution.py:40
  76.9 0.5 broadcast.372
  77.5 0.7 reduce.3
  78.2 9.0 %multiply_convert_fusion = bf16[512,16,512]{2,0,1:T(8,128)(2,1)} fusion(f32[512]{0:T(512)S(1)} %get-tuple-element.13, bf16[512,16,512]{2,0,1:T(8,128)(2,1)} %copy.17, pred[16,512]{1,0:T(8,128)(4,1)S(1)} %compare_and_fusion), kind=kLoop, calls=%fused_computation.3 | loop fusion | flops 16777216 | bytes 16787456 | tf_op jit(solution)/shard_map/convert_element_type | solution.py:41
  87.2 0.0 all-to-all-done.1
  87.2 6.2 %all-to-all-start = ((bf16[512,16,512]{2,0,1:T(8,128)(2,1)}), bf16[512,16,512]{2,0,1:T(8,128)(2,1)}, u32[]{:S(2)}, u32[]{:S(2)}) async-start(bf16[512,16,512]{2,0,1:T(8,128)(2,1)} %multiply_convert_fusion), calls=%async_computation | async-start | bytes 16777216 | tf_op jit(solution)/shard_map/all_to_all | solution.py:59
  93.5 0.1 select_reduce_fusion.1
  93.6 0.1 select_reduce_fusion
  93.8 0.6 gather_fusion.2
  94.3 0.6 copy.19
  95.0 182.6 %all-to-all-done = bf16[512,16,512]{2,0,1:T(8,128)(2,1)} async-done(((bf16[512,16,512]{2,0,1:T(8,128)(2,1)}), bf16[512,16,512]{2,0,1:T(8,128)(2,1)}, u32[]{:S(2)}, u32[]{:S(2)}) %all-to-all-start) | async-done | bytes 8388640 | tf_op jit(solution)/shard_map/all_to_all | solution.py:59
  277.6 8.3 %gather_fusion.1 = bf16[16,512,512]{2,1,0:T(8,128)(2,1)} fusion(bf16[16,512,512]{2,1,0:T(8,128)(2,1)} %bitcast.8, s32[1024]{0:T(1024)S(1)} %pad_clamp_fusion), kind=kCustom, calls=%fused_computation.1 | custom fusion | bytes 16777280 | tf_op jit(solution)/shard_map/gather | solution.py:67
  285.9 4.1 %fusion.212 = (bf16[2,512,512]{2,1,0:T(8,128)(2,1)S(1)}, bf16[2,512,512]{2,1,0:T(8,128)(2,1)S(1)}, bf16[2,512,512]{2,1,0:T(8,128)(2,1)S(1)}, bf16[2,512,512]{2,1...) fusion(bf16[16,512,512]{2,1,0:T(8,128)(2,1)} %gather_fusion.1), kind=kLoop, calls=%fused_computation.260 | loop fusion | bytes 16777216 | tf_op jit(solution)/shard_map/slice | solution.py:23
  290.0 5.3 %fusion.100 = f32[1024,512]{1,0:T(8,128)S(1)} fusion(bf16[1024,512]{1,0:T(8,128)(2,1)S(1)} %bitcast.59, s32[1024]{0:T(1024)S(1)} %iota_add_fusion.6, s32[1024]{0:T(1024)S(1)} %copy-done.2), kind=kOutput, calls=%fused_computation.122 | convolution fusion | flops 1091567616 | bytes 3153920 | tf_op jit(solution)/shard_map/dot_general | solution.py:21
  295.3 5.3 %fusion.88 = f32[1024,512]{1,0:T(8,128)S(1)} fusion(bf16[1024,512]{1,0:T(8,128)(2,1)S(1)} %bitcast.58, s32[1024]{0:T(1024)S(1)} %iota_add_fusion, s32[1024]{0:T(1024)S(1)} %copy-done.2), kind=kOutput, calls=%fused_computation.116 | convolution fusion | flops 1091567616 | bytes 3153920 | tf_op jit(solution)/shard_map/dot_general | solution.py:21
  300.5 5.5 %fusion.90 = f32[1024,512]{1,0:T(8,128)S(1)} fusion(bf16[1024,512]{1,0:T(8,128)(2,1)S(1)} %bitcast.57, s32[1024]{0:T(1024)S(1)} %iota_add_fusion.1, s32[1024]{0:T(1024)S(1)} %copy-done.2), kind=kOutput, calls=%fused_computation.117 | convolution fusion | flops 1091567616 | bytes 3153920 | tf_op jit(solution)/shard_map/dot_general | solution.py:21
  306.0 5.3 %fusion.92 = f32[1024,512]{1,0:T(8,128)S(1)} fusion(bf16[1024,512]{1,0:T(8,128)(2,1)S(1)} %bitcast.56, s32[1024]{0:T(1024)S(1)} %iota_add_fusion.2, s32[1024]{0:T(1024)S(1)} %copy-done.2), kind=kOutput, calls=%fused_computation.118 | convolution fusion | flops 1091567616 | bytes 3153920 | tf_op jit(solution)/shard_map/dot_general | solution.py:21
  311.3 5.7 %fusion.94 = f32[1024,512]{1,0:T(8,128)S(1)} fusion(bf16[1024,512]{1,0:T(8,128)(2,1)S(1)} %bitcast.55, s32[1024]{0:T(1024)S(1)} %iota_add_fusion.3, s32[1024]{0:T(1024)S(1)} %copy-done.2), kind=kOutput, calls=%fused_computation.119 | convolution fusion | flops 1091567616 | bytes 3153920 | tf_op jit(solution)/shard_map/dot_general | solution.py:21
  317.0 5.3 %fusion.96 = f32[1024,512]{1,0:T(8,128)S(1)} fusion(bf16[1024,512]{1,0:T(8,128)(2,1)S(1)} %bitcast.54, s32[1024]{0:T(1024)S(1)} %iota_add_fusion.4, s32[1024]{0:T(1024)S(1)} %copy-done.2), kind=kOutput, calls=%fused_computation.120 | convolution fusion | flops 1091567616 | bytes 3153920 | tf_op jit(solution)/shard_map/dot_general | solution.py:21
  322.3 5.5 %fusion.98 = f32[1024,512]{1,0:T(8,128)S(1)} fusion(bf16[1024,512]{1,0:T(8,128)(2,1)S(1)} %bitcast.53, s32[1024]{0:T(1024)S(1)} %iota_add_fusion.5, s32[1024]{0:T(1024)S(1)} %copy-done.2), kind=kOutput, calls=%fused_computation.121 | convolution fusion | flops 1091567616 | bytes 3153920 | tf_op jit(solution)/shard_map/dot_general | solution.py:21
  327.7 6.0 %add_add_fusion = f32[1024,512]{1,0:T(8,128)S(1)} fusion(f32[1024,512]{1,0:T(8,128)S(1)} %fusion.88, f32[1024,512]{1,0:T(8,128)S(1)} %fusion.90, f32[1024,512]{1,0:T(8,128)S(1)} %fusion.92, f32[1024,512]{1,0:T(8,128)S(1)} %fusion.94, f32[1024,512]{1,0:T(8,128)S(1)} %fusion.96, f32[1024,512]{1,0:T(8,128)S(1)} %fusion.98, f32[1024,512]{1,0:T(8,128)S(1)} %fusion.100, ...), kind=kOutput, calls=%fused_computation.125 | convolution fusion | flops 1095237632 | bytes 17833984 | tf_op jit(solution)/shard_map/dot_general | solution.py:21
  333.8 0.0 copy-start
  333.8 1.9 fusion.213
  335.6 31.4 %psum.15 = f32[1024]{0:T(1024)S(1)} all-reduce(f32[1024]{0:T(1024)S(1)} %bitcast.63), channel_id=1, replica_groups=mesh['section'=4,'expert'=2,'tensor'=4] {'section','tensor'}, use_global_device_ids=true, to_apply=%region_3.4 | all-reduce | flops 1024 | bytes 8192 | tf_op jit(solution)/shard_map/psum | solution.py:73
  367.0 0.6 broadcast_multiply_fusion
  (23 shorter events, 0.2 us)
Async XLA Ops:
  8.0 79.2 %all-to-all-start.1 = ((f32[16,1,512]{2,1,0:T(1,128)}), f32[16,1,512]{2,1,0:T(1,128)S(1)}, u32[]{:S(2)}, u32[]{:S(2)}) async-start(f32[16,1,512]{2,1,0:T(1,128)} %stack.2), calls=%async_computation.1 | async-start | bytes 65536 | tf_op jit(solution)/shard_map/all_to_all | solution.py:55
  14.4 12.0 %copy-start.1 = (s32[1,8192]{1,0:T(1,128)S(1)}, s32[1,8192]{1,0:T(1,128)}, u32[]{:S(2)}) copy-start(s32[1,8192]{1,0:T(1,128)} %param.7) | copy-start | bytes 98308
  87.2 6.3 %copy-start.3 = (s32[4]{0:T(128)S(1)}, s32[4]{0:T(128)}, u32[]{:S(2)}) copy-start(s32[4]{0:T(128)} %param.8) | copy-start | bytes 52
  87.2 190.4 %all-to-all-start = ((bf16[512,16,512]{2,0,1:T(8,128)(2,1)}), bf16[512,16,512]{2,0,1:T(8,128)(2,1)}, u32[]{:S(2)}, u32[]{:S(2)}) async-start(bf16[512,16,512]{2,0,1:T(8,128)(2,1)} %multiply_convert_fusion), calls=%async_computation | async-start | bytes 16777216 | tf_op jit(solution)/shard_map/all_to_all | solution.py:59
  285.9 4.1 %copy-start.2 = (s32[1024]{0:T(1024)S(1)}, s32[1024]{0:T(1024)}, u32[]{:S(2)}) copy-start(s32[1024]{0:T(1024)} %param.9) | copy-start | bytes 12292
  333.8 33.8 %copy-start = (f32[1024,512]{1,0:T(8,128)}, f32[1024,512]{1,0:T(8,128)S(1)}, u32[]{:S(2)}) copy-start(f32[1024,512]{1,0:T(8,128)S(1)} %add_add_fusion) | copy-start | bytes 6291460
